TPU v7x, 32 devices: a whole 2x2x4 slice. The times are simulated.
32 devices in a mesh: gx: 2 (over core), gy: 4 (over y, x), gz: 4 (over z).
Axes of the slice: x: 2, y: 2, z: 4, core: 2. Of those that a mesh axis runs over, the one named last changes fastest.
Arguments:
- queries: bfloat16 [128, 32, 128], P(None, 'gy'), may hold values from -6 to 6
- passages: bfloat16 [1024, 256, 128], P('gx', 'gz'), may hold values from -0.5 to 0.5
- passage_len: int32 [1024], P('gx'), may hold values from 32 to 256
- query_len: int32 [128], replicated, may hold values from 8 to 32
Outputs:
- log_probs: float32 [128, 1024], P(None, ('gx', 'gz'))
All inputs are finite; a program needn't handle non-finite values.
Results may differ from a plain program's by a relative error of at most 0.0003.
Values sent between devices are 32-bit elements; how exact they have to be, the bound alone decides.
No kernel may reach another device: no remote copies, remote signals or barrier semaphores. Data moves between devices by JAX's collectives and lax.ppermute only.
A program may use at most 64 MiB of HBM per device.

v0:
```python
import math
import jax
import jax.numpy as jnp
from jax import lax
from jax.sharding import PartitionSpec as P

masked_low = -1e30


def combined_all(array, axis, combine):
    everything = jax.tree.map(lambda part: lax.all_gather(part, axis), array)
    initial = jax.tree.map(lambda part: part[0], everything)

    def turn(k, so_far):
        return combine(so_far, jax.tree.map(lambda part: part[k], everything))

    return lax.fori_loop(1, lax.axis_size(axis), turn, initial)


def token_maxima(queries, passages, passage_len):
    query_count = queries.shape[0]
    query_rows = queries.shape[1]
    width = queries.shape[2]
    passage_count = passages.shape[0]
    token_count = passages.shape[1]
    flat_queries = queries.reshape(query_count * query_rows, width)
    per_block = math.gcd(passage_count, 32)
    num_blocks = passage_count // per_block
    token_ids = lax.axis_index("gz") * token_count + jnp.arange(token_count, dtype=jnp.int32)
    tile_stack = passages.reshape(num_blocks, per_block * token_count, width)
    length_stack = passage_len.reshape(num_blocks, per_block)

    def block_maxima(packed):
        passage_tile, tile_len = packed
        scores = lax.dot_general(
            flat_queries, passage_tile, (((1,), (1,)), ((), ())), preferred_element_type=jnp.float32
        )
        scores = scores.reshape(query_count * query_rows, per_block, token_count)
        usable = token_ids[None, :] < tile_len[:, None]
        scores = jnp.where(usable[None], scores, masked_low)
        return jnp.max(scores, axis=2)

    pieces = lax.map(block_maxima, (tile_stack, length_stack))
    return jnp.transpose(pieces, (1, 0, 2)).reshape(query_count, query_rows, passage_count)


def join_pairs(earlier, other_pair):
    highest = jnp.maximum(earlier[0], other_pair[0])
    summed = earlier[1] * jnp.exp(earlier[0] - highest) + other_pair[1] * jnp.exp(
        other_pair[0] - highest
    )
    return (highest, summed)


def fold_peers(received):
    return jnp.max(received, axis=2)


def shards(queries, passages, passage_len, query_len):
    maxima = token_maxima(queries, passages, passage_len)
    query_count = maxima.shape[0]
    query_rows = maxima.shape[1]
    passage_count = maxima.shape[2]
    query_ids = lax.axis_index("gy") * query_rows + jnp.arange(query_rows, dtype=jnp.int32)
    counted = (query_ids[None, :] < query_len[:, None])[:, :, None]
    spread = maxima.reshape(query_count, query_rows, 1, passage_count)
    merged = fold_peers(lax.all_to_all(spread, "gz", split_axis=3, concat_axis=2, tiled=True))
    partial_value = jnp.sum(jnp.where(counted, merged, 0.0), axis=1)
    scores_here = lax.psum(partial_value, "gy")
    local_top = jnp.max(scores_here, axis=1)
    local_sum = jnp.sum(jnp.exp(scores_here - local_top[:, None]), axis=1)
    highest, summed = combined_all((local_top, local_sum), ("gx", "gz"), join_pairs)
    return scores_here - (highest + jnp.log(summed))[:, None]


def solution(mesh):
    return jax.shard_map(
        shards,
        mesh=mesh,
        in_specs=(P(None, "gy", None), P("gx", "gz", None), P("gx"), P()),
        out_specs=P(None, ("gx", "gz")),
        check_vma=False,
    )
```

profile of v0, /device:TPU:1, one launch (start us, length us, event | category | flops | bytes accessed | tf_op | source)
XLA Modules:
  0.0 208.4 jit_solution(13668500045373860605)
XLA Ops:
  6.5 0.8 reshape.79
  7.3 40.6 %while.29 = (s32[]{:T(128)}, f32[16,1024,32]{1,2,0:T(8,128)S(1)}, s32[16,32]{1,0:T(8,128)S(1)}, bf16[16,2048,128]{2,1,0:T(8,128)(2,1)}, bf16[1024,128]{1,0:T(8,128)(2,1)}, /*index=5*/s32[]{:T(128)}, s32[]{:T(128)}) while((s32[]{:T(128)}, f32[16,1024,32]{1,2,0:T(8,128)S(1)}, s32[16,32]{1,0:T(8,128)S(1)}, ...), condition=%wide.region_2.3_spmd.clone, body=%wide.region_0.2_spmd.clone.sunk | while | flops 541034560 | bytes 1185241 | solution.py:43
  7.4 2.4 %select_reduce_fusion.3 = f32[1024,32]{0,1:T(8,128)S(1)} fusion(pred[32,64]{1,0:T(8,128)(4,1)S(1)} %broadcast_compare_fusion.3, bf16[1024,128]{1,0:T(8,128)(2,1)} %get-tuple-element.302, bf16[16,2048,128]{2,1,0:T(8,128)(2,1)} %get-tuple-element.301, s32[]{:T(128)} %get-tuple-element.291), kind=kOutput, calls=%fused_computation.7.clone.1 | convolution fusion | flops 541032448 | bytes 920064 | tf_op jit(solution)/shard_map/while/body/eval_jaxpr/dot_general | solution.py:35
  9.9 2.4 %select_reduce_fusion.3 = f32[1024,32]{0,1:T(8,128)S(1)} fusion(pred[32,64]{1,0:T(8,128)(4,1)S(1)} %broadcast_compare_fusion.3, bf16[1024,128]{1,0:T(8,128)(2,1)} %get-tuple-element.302, bf16[16,2048,128]{2,1,0:T(8,128)(2,1)} %get-tuple-element.301, s32[]{:T(128)} %get-tuple-element.291), kind=kOutput, calls=%fused_computation.7.clone.1 | convolution fusion | flops 541032448 | bytes 920064 | tf_op jit(solution)/shard_map/while/body/eval_jaxpr/dot_general | solution.py:35
  12.5 2.4 %select_reduce_fusion.3 = f32[1024,32]{0,1:T(8,128)S(1)} fusion(pred[32,64]{1,0:T(8,128)(4,1)S(1)} %broadcast_compare_fusion.3, bf16[1024,128]{1,0:T(8,128)(2,1)} %get-tuple-element.302, bf16[16,2048,128]{2,1,0:T(8,128)(2,1)} %get-tuple-element.301, s32[]{:T(128)} %get-tuple-element.291), kind=kOutput, calls=%fused_computation.7.clone.1 | convolution fusion | flops 541032448 | bytes 920064 | tf_op jit(solution)/shard_map/while/body/eval_jaxpr/dot_general | solution.py:35
  15.0 2.4 %select_reduce_fusion.3 = f32[1024,32]{0,1:T(8,128)S(1)} fusion(pred[32,64]{1,0:T(8,128)(4,1)S(1)} %broadcast_compare_fusion.3, bf16[1024,128]{1,0:T(8,128)(2,1)} %get-tuple-element.302, bf16[16,2048,128]{2,1,0:T(8,128)(2,1)} %get-tuple-element.301, s32[]{:T(128)} %get-tuple-element.291), kind=kOutput, calls=%fused_computation.7.clone.1 | convolution fusion | flops 541032448 | bytes 920064 | tf_op jit(solution)/shard_map/while/body/eval_jaxpr/dot_general | solution.py:35
  17.5 2.4 %select_reduce_fusion.3 = f32[1024,32]{0,1:T(8,128)S(1)} fusion(pred[32,64]{1,0:T(8,128)(4,1)S(1)} %broadcast_compare_fusion.3, bf16[1024,128]{1,0:T(8,128)(2,1)} %get-tuple-element.302, bf16[16,2048,128]{2,1,0:T(8,128)(2,1)} %get-tuple-element.301, s32[]{:T(128)} %get-tuple-element.291), kind=kOutput, calls=%fused_computation.7.clone.1 | convolution fusion | flops 541032448 | bytes 920064 | tf_op jit(solution)/shard_map/while/body/eval_jaxpr/dot_general | solution.py:35
  20.1 2.4 %select_reduce_fusion.3 = f32[1024,32]{0,1:T(8,128)S(1)} fusion(pred[32,64]{1,0:T(8,128)(4,1)S(1)} %broadcast_compare_fusion.3, bf16[1024,128]{1,0:T(8,128)(2,1)} %get-tuple-element.302, bf16[16,2048,128]{2,1,0:T(8,128)(2,1)} %get-tuple-element.301, s32[]{:T(128)} %get-tuple-element.291), kind=kOutput, calls=%fused_computation.7.clone.1 | convolution fusion | flops 541032448 | bytes 920064 | tf_op jit(solution)/shard_map/while/body/eval_jaxpr/dot_general | solution.py:35
  22.6 2.4 %select_reduce_fusion.3 = f32[1024,32]{0,1:T(8,128)S(1)} fusion(pred[32,64]{1,0:T(8,128)(4,1)S(1)} %broadcast_compare_fusion.3, bf16[1024,128]{1,0:T(8,128)(2,1)} %get-tuple-element.302, bf16[16,2048,128]{2,1,0:T(8,128)(2,1)} %get-tuple-element.301, s32[]{:T(128)} %get-tuple-element.291), kind=kOutput, calls=%fused_computation.7.clone.1 | convolution fusion | flops 541032448 | bytes 920064 | tf_op jit(solution)/shard_map/while/body/eval_jaxpr/dot_general | solution.py:35
  25.2 2.4 %select_reduce_fusion.3 = f32[1024,32]{0,1:T(8,128)S(1)} fusion(pred[32,64]{1,0:T(8,128)(4,1)S(1)} %broadcast_compare_fusion.3, bf16[1024,128]{1,0:T(8,128)(2,1)} %get-tuple-element.302, bf16[16,2048,128]{2,1,0:T(8,128)(2,1)} %get-tuple-element.301, s32[]{:T(128)} %get-tuple-element.291), kind=kOutput, calls=%fused_computation.7.clone.1 | convolution fusion | flops 541032448 | bytes 920064 | tf_op jit(solution)/shard_map/while/body/eval_jaxpr/dot_general | solution.py:35
  27.7 2.4 %select_reduce_fusion.3 = f32[1024,32]{0,1:T(8,128)S(1)} fusion(pred[32,64]{1,0:T(8,128)(4,1)S(1)} %broadcast_compare_fusion.3, bf16[1024,128]{1,0:T(8,128)(2,1)} %get-tuple-element.302, bf16[16,2048,128]{2,1,0:T(8,128)(2,1)} %get-tuple-element.301, s32[]{:T(128)} %get-tuple-element.291), kind=kOutput, calls=%fused_computation.7.clone.1 | convolution fusion | flops 541032448 | bytes 920064 | tf_op jit(solution)/shard_map/while/body/eval_jaxpr/dot_general | solution.py:35
  30.2 2.4 %select_reduce_fusion.3 = f32[1024,32]{0,1:T(8,128)S(1)} fusion(pred[32,64]{1,0:T(8,128)(4,1)S(1)} %broadcast_compare_fusion.3, bf16[1024,128]{1,0:T(8,128)(2,1)} %get-tuple-element.302, bf16[16,2048,128]{2,1,0:T(8,128)(2,1)} %get-tuple-element.301, s32[]{:T(128)} %get-tuple-element.291), kind=kOutput, calls=%fused_computation.7.clone.1 | convolution fusion | flops 541032448 | bytes 920064 | tf_op jit(solution)/shard_map/while/body/eval_jaxpr/dot_general | solution.py:35
  32.8 2.4 %select_reduce_fusion.3 = f32[1024,32]{0,1:T(8,128)S(1)} fusion(pred[32,64]{1,0:T(8,128)(4,1)S(1)} %broadcast_compare_fusion.3, bf16[1024,128]{1,0:T(8,128)(2,1)} %get-tuple-element.302, bf16[16,2048,128]{2,1,0:T(8,128)(2,1)} %get-tuple-element.301, s32[]{:T(128)} %get-tuple-element.291), kind=kOutput, calls=%fused_computation.7.clone.1 | convolution fusion | flops 541032448 | bytes 920064 | tf_op jit(solution)/shard_map/while/body/eval_jaxpr/dot_general | solution.py:35
  35.3 2.4 %select_reduce_fusion.3 = f32[1024,32]{0,1:T(8,128)S(1)} fusion(pred[32,64]{1,0:T(8,128)(4,1)S(1)} %broadcast_compare_fusion.3, bf16[1024,128]{1,0:T(8,128)(2,1)} %get-tuple-element.302, bf16[16,2048,128]{2,1,0:T(8,128)(2,1)} %get-tuple-element.301, s32[]{:T(128)} %get-tuple-element.291), kind=kOutput, calls=%fused_computation.7.clone.1 | convolution fusion | flops 541032448 | bytes 920064 | tf_op jit(solution)/shard_map/while/body/eval_jaxpr/dot_general | solution.py:35
  37.8 2.4 %select_reduce_fusion.3 = f32[1024,32]{0,1:T(8,128)S(1)} fusion(pred[32,64]{1,0:T(8,128)(4,1)S(1)} %broadcast_compare_fusion.3, bf16[1024,128]{1,0:T(8,128)(2,1)} %get-tuple-element.302, bf16[16,2048,128]{2,1,0:T(8,128)(2,1)} %get-tuple-element.301, s32[]{:T(128)} %get-tuple-element.291), kind=kOutput, calls=%fused_computation.7.clone.1 | convolution fusion | flops 541032448 | bytes 920064 | tf_op jit(solution)/shard_map/while/body/eval_jaxpr/dot_general | solution.py:35
  40.4 2.4 %select_reduce_fusion.3 = f32[1024,32]{0,1:T(8,128)S(1)} fusion(pred[32,64]{1,0:T(8,128)(4,1)S(1)} %broadcast_compare_fusion.3, bf16[1024,128]{1,0:T(8,128)(2,1)} %get-tuple-element.302, bf16[16,2048,128]{2,1,0:T(8,128)(2,1)} %get-tuple-element.301, s32[]{:T(128)} %get-tuple-element.291), kind=kOutput, calls=%fused_computation.7.clone.1 | convolution fusion | flops 541032448 | bytes 920064 | tf_op jit(solution)/shard_map/while/body/eval_jaxpr/dot_general | solution.py:35
  42.9 2.4 %select_reduce_fusion.3 = f32[1024,32]{0,1:T(8,128)S(1)} fusion(pred[32,64]{1,0:T(8,128)(4,1)S(1)} %broadcast_compare_fusion.3, bf16[1024,128]{1,0:T(8,128)(2,1)} %get-tuple-element.302, bf16[16,2048,128]{2,1,0:T(8,128)(2,1)} %get-tuple-element.301, s32[]{:T(128)} %get-tuple-element.291), kind=kOutput, calls=%fused_computation.7.clone.1 | convolution fusion | flops 541032448 | bytes 920064 | tf_op jit(solution)/shard_map/while/body/eval_jaxpr/dot_general | solution.py:35
  45.5 2.4 %select_reduce_fusion.3 = f32[1024,32]{0,1:T(8,128)S(1)} fusion(pred[32,64]{1,0:T(8,128)(4,1)S(1)} %broadcast_compare_fusion.3, bf16[1024,128]{1,0:T(8,128)(2,1)} %get-tuple-element.302, bf16[16,2048,128]{2,1,0:T(8,128)(2,1)} %get-tuple-element.301, s32[]{:T(128)} %get-tuple-element.291), kind=kOutput, calls=%fused_computation.7.clone.1 | convolution fusion | flops 541032448 | bytes 920064 | tf_op jit(solution)/shard_map/while/body/eval_jaxpr/dot_general | solution.py:35
  47.9 6.2 %copy.11 = f32[1024,16,32]{2,1,0:T(8,128)} copy(f32[1024,16,32]{0,2,1:T(8,128)S(1)} %bitcast.51) | data formatting | bytes 4194304 | tf_op jit(solution)/shard_map/transpose | solution.py:44
  54.1 6.2 %reshape_reshape.3 = f32[128,8,1,512]{3,1,0,2:T(8,128)S(1)} reshape(f32[1024,16,32]{2,1,0:T(8,128)} %copy.11) | data formatting | bytes 4194304 | tf_op jit(solution)/shard_map/reshape;reshape | solution.py:66
  60.4 2.1 copy.12
  62.5 5.5 %all-to-all-start = ((f32[128,8,1,512]{0,1,2,3:T(8,128)}), f32[128,8,1,512]{0,1,2,3:T(8,128)S(1)}, u32[]{:S(2)}, u32[]{:S(2)}) async-start(f32[128,8,1,512]{0,1,2,3:T(8,128)} %copy.12), calls=%async_computation | async-start | bytes 4194304 | tf_op jit(solution)/shard_map/all_to_all | solution.py:67
  68.1 47.6 %all-to-all-done = f32[128,8,1,512]{0,1,2,3:T(8,128)S(1)} async-done(((f32[128,8,1,512]{0,1,2,3:T(8,128)}), f32[128,8,1,512]{0,1,2,3:T(8,128)S(1)}, u32[]{:S(2)}, u32[]{:S(2)}) %all-to-all-start) | async-done | bytes 2097184 | tf_op jit(solution)/shard_map/all_to_all | solution.py:67
  115.9 4.8 %copy.15 = f32[128,8,128]{1,0,2:T(8,128)} copy(f32[128,8,128]{0,1,2:T(8,128)S(1)} %reduce_max.27) | data formatting | bytes 1048576
  120.8 6.2 %select_reduce_fusion.1 = f32[128,128]{0,1:T(8,128)} fusion(f32[128,8,128]{1,0,2:T(8,128)} %copy.15, pred[128,8]{1,0:T(8,128)(4,1)S(1)} %broadcast_compare_fusion.1), kind=kLoop, calls=%fused_computation.17 | loop fusion | flops 245760 | bytes 590848 | tf_op jit(solution)/shard_map/reduce_sum | solution.py:68
  127.0 41.4 %all-reduce.2.cloned.1.call-done = f32[128,128]{0,1:T(8,128)} async-done(((f32[128,128]{0,1:T(8,128)}), f32[128,128]{0,1:T(8,128)}) %all-reduce.2.cloned.1.call-update) | async-done | bytes 65552 | tf_op jit(solution)/shard_map/psum | solution.py:69
  168.4 0.9 reduce_max.28
  169.3 0.9 exponential_reduce_fusion
  170.2 16.8 %all-gather.3 = f32[8,1,128]{2,1,0:T(1,128)S(1)} all-gather(f32[1,1,128]{2,1,0:T(1,128)S(1)} %bitcast.55), channel_id=3, replica_groups=mesh['gx'=2,'gy'=4,'gz'=4] {'gx','gz'}, dimensions={0}, use_global_device_ids=true | all-gather | bytes 4608 | tf_op jit(solution)/shard_map/all_gather | solution.py:11
  186.9 12.8 %all-gather.2 = f32[8,1,128]{2,1,0:T(1,128)S(1)} all-gather(f32[1,1,128]{2,1,0:T(1,128)S(1)} %bitcast.54), channel_id=2, replica_groups=mesh['gx'=2,'gy'=4,'gz'=4] {'gx','gz'}, dimensions={0}, use_global_device_ids=true | all-gather | bytes 4608 | tf_op jit(solution)/shard_map/all_gather | solution.py:11
  200.0 0.8 broadcast_subtract_fusion
  200.9 0.7 copy.14
  (83 shorter events, 2.4 us)
Async XLA Ops:
  62.5 5.6 %copy-start = (s32[128]{0:T(128)S(1)}, s32[128]{0:T(128)}, u32[]{:S(2)}) copy-start(s32[128]{0:T(128)} %param.11) | copy-start | bytes 1540
  62.5 53.3 %all-to-all-start = ((f32[128,8,1,512]{0,1,2,3:T(8,128)}), f32[128,8,1,512]{0,1,2,3:T(8,128)S(1)}, u32[]{:S(2)}, u32[]{:S(2)}) async-start(f32[128,8,1,512]{0,1,2,3:T(8,128)} %copy.12), calls=%async_computation | async-start | bytes 4194304 | tf_op jit(solution)/shard_map/all_to_all | solution.py:67
  68.0 100.4 %all-reduce.2.cloned.1.call-start = ((), (), s32[]{:S(2)}) async-start(), calls=%async_computation.1 | async-start | bytes 131072 | tf_op jit(solution)/shard_map/psum | solution.py:69
Sparse Core Ops, SparseCore 0:
  127.2 41.2 all-reduce.1
where the time goes:
time: 209 us; the launch traced here: 208 us
  waiting for transfers between devices  89 us (43%)
  matrix products  38.2 us (18%)
  blocking collectives  29.5 us (14%)
  local copies, waits for them, and re-layouts  21.3 us (10%)
  between operations  13.4 us (6%)
  other arithmetic  10.6 us (5%)
  starting transfers between devices  5.54 us (3%)
    all_to_all x1, waiting for transfers between devices, shards(): lax.all_to_all(spread, 'gz', split_axis=3, concat_axis=2, tiled=True)  47.6 us
    psum x1, waiting for transfers between devices, shards(): scores_here = lax.psum(partial_value, 'gy')  41.4 us
    dot_general x16, matrix products, block_maxima(): lax.dot_general(flat_queries, passage_tile, (((1,), (1,)), ((), ())), pre...  38.2 us
    all_gather x2, blocking collectives, combined_all(): everything = jax.tree.map(lambda part: lax.all_gather(part, axis), array)  29.5 us
    another operation x2, local copies, waits for them, and re-layouts, shards(): spread = maxima.reshape(query_count, query_rows, 1, passage_count)  8.32 us
    reduce_sum x1, other arithmetic, shards(): partial_value = jnp.sum(jnp.where(counted, merged, 0.0), axis=1)  6.25 us
    transpose x1, local copies, waits for them, and re-layouts, token_maxima(): jnp.transpose(pieces, (1, 0, 2))  6.23 us
    all_to_all x1, starting transfers between devices, shards(): lax.all_to_all(spread, 'gz', split_axis=3, concat_axis=2, tiled=True)  5.54 us
  transfers between devices with their start and end apart: 2, of which 2 were waited for; matrix products, arithmetic and copies ran while one was open for 0% of the time, Pallas kernels for 0%

commit v1 on v0

--- a/solution.py
+++ b/solution.py
@@ -66,7 +66,7 @@
     spread = maxima.reshape(query_count, query_rows, 1, passage_count)
     merged = fold_peers(lax.all_to_all(spread, "gz", split_axis=3, concat_axis=2, tiled=True))
     partial_value = jnp.sum(jnp.where(counted, merged, 0.0), axis=1)
-    scores_here = lax.psum(partial_value, "gy")
+    scores_here = jnp.sum(lax.all_gather(partial_value, "gy"), axis=0)
     local_top = jnp.max(scores_here, axis=1)
     local_sum = jnp.sum(jnp.exp(scores_here - local_top[:, None]), axis=1)
     highest, summed = combined_all((local_top, local_sum), ("gx", "gz"), join_pairs)

time: 209 us -> 161 us (0.77)
  waiting for transfers between devices: 89 us -> 47.7 us
  between operations: 13.4 us -> 0.07 us
  blocking collectives: 29.5 us -> 38.8 us
  other arithmetic: 10.6 us -> 7.58 us
    psum x1 -> x0, waiting for transfers between devices: 41.4 us -> none  [shards(): scores_here = lax.psum(partial_value, 'gy')]
    all_gather x0 -> x1, blocking collectives: none -> 8.02 us  [shards(): scores_here = jnp.sum(lax.all_gather(partial_value, 'gy'), axis=0)]
  transfers between devices with their start and end apart: 2 -> 1, of which waited for: 2 -> 1; matrix products, arithmetic and copies ran while one was open for 0% -> 0% of each run, Pallas kernels for 0% -> 0%
where the time goes in v1:
time: 161 us; the launch traced here: 160 us
  waiting for transfers between devices  47.7 us (30%)
  blocking collectives  38.8 us (24%)
  matrix products  38.2 us (24%)
  local copies, waits for them, and re-layouts  21.4 us (13%)
  other arithmetic  7.58 us (5%)
  starting transfers between devices  5.54 us (3%)
    all_to_all x1, waiting for transfers between devices, shards(): lax.all_to_all(spread, 'gz', split_axis=3, concat_axis=2, tiled=True)  47.7 us
    dot_general x16, matrix products, block_maxima(): lax.dot_general(flat_queries, passage_tile, (((1,), (1,)), ((), ())), pre...  38.2 us
    all_gather x2, blocking collectives, combined_all(): everything = jax.tree.map(lambda part: lax.all_gather(part, axis), array)  30.8 us
    another operation x2, local copies, waits for them, and re-layouts, shards(): spread = maxima.reshape(query_count, query_rows, 1, passage_count)  8.32 us
    all_gather x1, blocking collectives, shards(): scores_here = jnp.sum(lax.all_gather(partial_value, 'gy'), axis=0)  8.02 us
    transpose x1, local copies, waits for them, and re-layouts, token_maxima(): jnp.transpose(pieces, (1, 0, 2))  6.23 us
    reduce_sum x1, other arithmetic, shards(): partial_value = jnp.sum(jnp.where(counted, merged, 0.0), axis=1)  5.61 us
    all_to_all x1, starting transfers between devices, shards(): lax.all_to_all(spread, 'gz', split_axis=3, concat_axis=2, tiled=True)  5.54 us
  transfers between devices with their start and end apart: 1, of which 1 were waited for; matrix products, arithmetic and copies ran while one was open for 0% of the time, Pallas kernels for 0%

profile of v1, /device:TPU:1, one launch (start us, length us, event | category | flops | bytes accessed | tf_op | source)
XLA Modules:
  0.0 160.0 jit_solution(12179070466506518602)
XLA Ops:
  0.0 0.8 reshape.79
  0.8 40.5 %while.29 = (s32[]{:T(128)}, f32[16,1024,32]{1,2,0:T(8,128)S(1)}, s32[16,32]{1,0:T(8,128)S(1)}, bf16[16,2048,128]{2,1,0:T(8,128)(2,1)}, bf16[1024,128]{1,0:T(8,128)(2,1)}, /*index=5*/s32[]{:T(128)}, s32[]{:T(128)}) while((s32[]{:T(128)}, f32[16,1024,32]{1,2,0:T(8,128)S(1)}, s32[16,32]{1,0:T(8,128)S(1)}, ...), condition=%wide.region_2.3_spmd.clone, body=%wide.region_0.2_spmd.clone.sunk | while | flops 541034560 | bytes 1185241 | solution.py:43
  0.8 2.4 %select_reduce_fusion.3 = f32[1024,32]{0,1:T(8,128)S(1)} fusion(pred[32,64]{1,0:T(8,128)(4,1)S(1)} %broadcast_compare_fusion.3, bf16[1024,128]{1,0:T(8,128)(2,1)} %get-tuple-element.302, bf16[16,2048,128]{2,1,0:T(8,128)(2,1)} %get-tuple-element.301, s32[]{:T(128)} %get-tuple-element.291), kind=kOutput, calls=%fused_computation.7.clone.1 | convolution fusion | flops 541032448 | bytes 920064 | tf_op jit(solution)/shard_map/while/body/eval_jaxpr/dot_general | solution.py:35
  3.4 2.4 %select_reduce_fusion.3 = f32[1024,32]{0,1:T(8,128)S(1)} fusion(pred[32,64]{1,0:T(8,128)(4,1)S(1)} %broadcast_compare_fusion.3, bf16[1024,128]{1,0:T(8,128)(2,1)} %get-tuple-element.302, bf16[16,2048,128]{2,1,0:T(8,128)(2,1)} %get-tuple-element.301, s32[]{:T(128)} %get-tuple-element.291), kind=kOutput, calls=%fused_computation.7.clone.1 | convolution fusion | flops 541032448 | bytes 920064 | tf_op jit(solution)/shard_map/while/body/eval_jaxpr/dot_general | solution.py:35
  5.9 2.4 %select_reduce_fusion.3 = f32[1024,32]{0,1:T(8,128)S(1)} fusion(pred[32,64]{1,0:T(8,128)(4,1)S(1)} %broadcast_compare_fusion.3, bf16[1024,128]{1,0:T(8,128)(2,1)} %get-tuple-element.302, bf16[16,2048,128]{2,1,0:T(8,128)(2,1)} %get-tuple-element.301, s32[]{:T(128)} %get-tuple-element.291), kind=kOutput, calls=%fused_computation.7.clone.1 | convolution fusion | flops 541032448 | bytes 920064 | tf_op jit(solution)/shard_map/while/body/eval_jaxpr/dot_general | solution.py:35
  8.4 2.4 %select_reduce_fusion.3 = f32[1024,32]{0,1:T(8,128)S(1)} fusion(pred[32,64]{1,0:T(8,128)(4,1)S(1)} %broadcast_compare_fusion.3, bf16[1024,128]{1,0:T(8,128)(2,1)} %get-tuple-element.302, bf16[16,2048,128]{2,1,0:T(8,128)(2,1)} %get-tuple-element.301, s32[]{:T(128)} %get-tuple-element.291), kind=kOutput, calls=%fused_computation.7.clone.1 | convolution fusion | flops 541032448 | bytes 920064 | tf_op jit(solution)/shard_map/while/body/eval_jaxpr/dot_general | solution.py:35
  11.0 2.4 %select_reduce_fusion.3 = f32[1024,32]{0,1:T(8,128)S(1)} fusion(pred[32,64]{1,0:T(8,128)(4,1)S(1)} %broadcast_compare_fusion.3, bf16[1024,128]{1,0:T(8,128)(2,1)} %get-tuple-element.302, bf16[16,2048,128]{2,1,0:T(8,128)(2,1)} %get-tuple-element.301, s32[]{:T(128)} %get-tuple-element.291), kind=kOutput, calls=%fused_computation.7.clone.1 | convolution fusion | flops 541032448 | bytes 920064 | tf_op jit(solution)/shard_map/while/body/eval_jaxpr/dot_general | solution.py:35
  13.5 2.4 %select_reduce_fusion.3 = f32[1024,32]{0,1:T(8,128)S(1)} fusion(pred[32,64]{1,0:T(8,128)(4,1)S(1)} %broadcast_compare_fusion.3, bf16[1024,128]{1,0:T(8,128)(2,1)} %get-tuple-element.302, bf16[16,2048,128]{2,1,0:T(8,128)(2,1)} %get-tuple-element.301, s32[]{:T(128)} %get-tuple-element.291), kind=kOutput, calls=%fused_computation.7.clone.1 | convolution fusion | flops 541032448 | bytes 920064 | tf_op jit(solution)/shard_map/while/body/eval_jaxpr/dot_general | solution.py:35
  16.1 2.4 %select_reduce_fusion.3 = f32[1024,32]{0,1:T(8,128)S(1)} fusion(pred[32,64]{1,0:T(8,128)(4,1)S(1)} %broadcast_compare_fusion.3, bf16[1024,128]{1,0:T(8,128)(2,1)} %get-tuple-element.302, bf16[16,2048,128]{2,1,0:T(8,128)(2,1)} %get-tuple-element.301, s32[]{:T(128)} %get-tuple-element.291), kind=kOutput, calls=%fused_computation.7.clone.1 | convolution fusion | flops 541032448 | bytes 920064 | tf_op jit(solution)/shard_map/while/body/eval_jaxpr/dot_general | solution.py:35
  18.6 2.4 %select_reduce_fusion.3 = f32[1024,32]{0,1:T(8,128)S(1)} fusion(pred[32,64]{1,0:T(8,128)(4,1)S(1)} %broadcast_compare_fusion.3, bf16[1024,128]{1,0:T(8,128)(2,1)} %get-tuple-element.302, bf16[16,2048,128]{2,1,0:T(8,128)(2,1)} %get-tuple-element.301, s32[]{:T(128)} %get-tuple-element.291), kind=kOutput, calls=%fused_computation.7.clone.1 | convolution fusion | flops 541032448 | bytes 920064 | tf_op jit(solution)/shard_map/while/body/eval_jaxpr/dot_general | solution.py:35
  21.1 2.4 %select_reduce_fusion.3 = f32[1024,32]{0,1:T(8,128)S(1)} fusion(pred[32,64]{1,0:T(8,128)(4,1)S(1)} %broadcast_compare_fusion.3, bf16[1024,128]{1,0:T(8,128)(2,1)} %get-tuple-element.302, bf16[16,2048,128]{2,1,0:T(8,128)(2,1)} %get-tuple-element.301, s32[]{:T(128)} %get-tuple-element.291), kind=kOutput, calls=%fused_computation.7.clone.1 | convolution fusion | flops 541032448 | bytes 920064 | tf_op jit(solution)/shard_map/while/body/eval_jaxpr/dot_general | solution.py:35
  23.7 2.4 %select_reduce_fusion.3 = f32[1024,32]{0,1:T(8,128)S(1)} fusion(pred[32,64]{1,0:T(8,128)(4,1)S(1)} %broadcast_compare_fusion.3, bf16[1024,128]{1,0:T(8,128)(2,1)} %get-tuple-element.302, bf16[16,2048,128]{2,1,0:T(8,128)(2,1)} %get-tuple-element.301, s32[]{:T(128)} %get-tuple-element.291), kind=kOutput, calls=%fused_computation.7.clone.1 | convolution fusion | flops 541032448 | bytes 920064 | tf_op jit(solution)/shard_map/while/body/eval_jaxpr/dot_general | solution.py:35
  26.2 2.4 %select_reduce_fusion.3 = f32[1024,32]{0,1:T(8,128)S(1)} fusion(pred[32,64]{1,0:T(8,128)(4,1)S(1)} %broadcast_compare_fusion.3, bf16[1024,128]{1,0:T(8,128)(2,1)} %get-tuple-element.302, bf16[16,2048,128]{2,1,0:T(8,128)(2,1)} %get-tuple-element.301, s32[]{:T(128)} %get-tuple-element.291), kind=kOutput, calls=%fused_computation.7.clone.1 | convolution fusion | flops 541032448 | bytes 920064 | tf_op jit(solution)/shard_map/while/body/eval_jaxpr/dot_general | solution.py:35
  28.7 2.4 %select_reduce_fusion.3 = f32[1024,32]{0,1:T(8,128)S(1)} fusion(pred[32,64]{1,0:T(8,128)(4,1)S(1)} %broadcast_compare_fusion.3, bf16[1024,128]{1,0:T(8,128)(2,1)} %get-tuple-element.302, bf16[16,2048,128]{2,1,0:T(8,128)(2,1)} %get-tuple-element.301, s32[]{:T(128)} %get-tuple-element.291), kind=kOutput, calls=%fused_computation.7.clone.1 | convolution fusion | flops 541032448 | bytes 920064 | tf_op jit(solution)/shard_map/while/body/eval_jaxpr/dot_general | solution.py:35
  31.3 2.4 %select_reduce_fusion.3 = f32[1024,32]{0,1:T(8,128)S(1)} fusion(pred[32,64]{1,0:T(8,128)(4,1)S(1)} %broadcast_compare_fusion.3, bf16[1024,128]{1,0:T(8,128)(2,1)} %get-tuple-element.302, bf16[16,2048,128]{2,1,0:T(8,128)(2,1)} %get-tuple-element.301, s32[]{:T(128)} %get-tuple-element.291), kind=kOutput, calls=%fused_computation.7.clone.1 | convolution fusion | flops 541032448 | bytes 920064 | tf_op jit(solution)/shard_map/while/body/eval_jaxpr/dot_general | solution.py:35
  33.8 2.4 %select_reduce_fusion.3 = f32[1024,32]{0,1:T(8,128)S(1)} fusion(pred[32,64]{1,0:T(8,128)(4,1)S(1)} %broadcast_compare_fusion.3, bf16[1024,128]{1,0:T(8,128)(2,1)} %get-tuple-element.302, bf16[16,2048,128]{2,1,0:T(8,128)(2,1)} %get-tuple-element.301, s32[]{:T(128)} %get-tuple-element.291), kind=kOutput, calls=%fused_computation.7.clone.1 | convolution fusion | flops 541032448 | bytes 920064 | tf_op jit(solution)/shard_map/while/body/eval_jaxpr/dot_general | solution.py:35
  36.3 2.4 %select_reduce_fusion.3 = f32[1024,32]{0,1:T(8,128)S(1)} fusion(pred[32,64]{1,0:T(8,128)(4,1)S(1)} %broadcast_compare_fusion.3, bf16[1024,128]{1,0:T(8,128)(2,1)} %get-tuple-element.302, bf16[16,2048,128]{2,1,0:T(8,128)(2,1)} %get-tuple-element.301, s32[]{:T(128)} %get-tuple-element.291), kind=kOutput, calls=%fused_computation.7.clone.1 | convolution fusion | flops 541032448 | bytes 920064 | tf_op jit(solution)/shard_map/while/body/eval_jaxpr/dot_general | solution.py:35
  38.9 2.4 %select_reduce_fusion.3 = f32[1024,32]{0,1:T(8,128)S(1)} fusion(pred[32,64]{1,0:T(8,128)(4,1)S(1)} %broadcast_compare_fusion.3, bf16[1024,128]{1,0:T(8,128)(2,1)} %get-tuple-element.302, bf16[16,2048,128]{2,1,0:T(8,128)(2,1)} %get-tuple-element.301, s32[]{:T(128)} %get-tuple-element.291), kind=kOutput, calls=%fused_computation.7.clone.1 | convolution fusion | flops 541032448 | bytes 920064 | tf_op jit(solution)/shard_map/while/body/eval_jaxpr/dot_general | solution.py:35
  41.3 6.2 %copy.14 = f32[1024,16,32]{2,1,0:T(8,128)} copy(f32[1024,16,32]{0,2,1:T(8,128)S(1)} %bitcast.53) | data formatting | bytes 4194304 | tf_op jit(solution)/shard_map/transpose | solution.py:44
  47.5 6.2 %reshape_reshape.3 = f32[128,8,1,512]{3,1,0,2:T(8,128)S(1)} reshape(f32[1024,16,32]{2,1,0:T(8,128)} %copy.14) | data formatting | bytes 4194304 | tf_op jit(solution)/shard_map/reshape;reshape | solution.py:66
  53.8 2.1 %copy.15 = f32[128,8,1,512]{0,1,2,3:T(8,128)} copy(f32[128,8,1,512]{3,1,0,2:T(8,128)S(1)} %reshape_reshape.3) | data formatting | bytes 4194304 | tf_op jit(solution)/shard_map/reshape;reshape | solution.py:66
  55.9 5.5 %all-to-all-start = ((f32[128,8,1,512]{0,1,2,3:T(8,128)}), f32[128,8,1,512]{0,1,2,3:T(8,128)S(1)}, u32[]{:S(2)}, u32[]{:S(2)}) async-start(f32[128,8,1,512]{0,1,2,3:T(8,128)} %copy.15), calls=%async_computation | async-start | bytes 4194304 | tf_op jit(solution)/shard_map/all_to_all | solution.py:67
  61.5 47.7 %all-to-all-done = f32[128,8,1,512]{0,1,2,3:T(8,128)S(1)} async-done(((f32[128,8,1,512]{0,1,2,3:T(8,128)}), f32[128,8,1,512]{0,1,2,3:T(8,128)S(1)}, u32[]{:S(2)}, u32[]{:S(2)}) %all-to-all-start) | async-done | bytes 2097184 | tf_op jit(solution)/shard_map/all_to_all | solution.py:67
  109.2 0.2 reduce_max.27
  109.4 4.8 %copy.18 = f32[128,8,128]{1,0,2:T(8,128)} copy(f32[128,8,128]{0,1,2:T(8,128)S(1)} %reduce_max.27) | data formatting | bytes 1048576
  114.2 5.6 %select_reduce_fusion.1 = f32[128,128]{0,1:T(8,128)S(1)} fusion(f32[128,8,128]{1,0,2:T(8,128)} %copy.18, pred[128,8]{1,0:T(8,128)(4,1)S(1)} %broadcast_compare_fusion.1), kind=kLoop, calls=%fused_computation.17 | loop fusion | flops 245760 | bytes 590848 | tf_op jit(solution)/shard_map/reduce_sum | solution.py:68
  119.8 8.0 %all-gather = f32[512,128]{0,1:T(8,128)S(1)} all-gather(f32[128,128]{0,1:T(8,128)S(1)} %select_reduce_fusion.1), channel_id=2, replica_groups=mesh['gx'=2,'gy'=4,'gz'=4] {'gy'}, dimensions={0}, use_global_device_ids=true | all-gather | bytes 327680 | tf_op jit(solution)/shard_map/all_gather | solution.py:69
  127.9 0.2 reduce_sum.28
  128.2 17.2 %all-gather.4 = f32[8,1,128]{2,1,0:T(1,128)S(1)} all-gather(f32[1,1,128]{2,1,0:T(1,128)S(1)} %bitcast.57), channel_id=4, replica_groups=mesh['gx'=2,'gy'=4,'gz'=4] {'gx','gz'}, dimensions={0}, use_global_device_ids=true | all-gather | bytes 4608 | tf_op jit(solution)/shard_map/all_gather | solution.py:11
  145.4 13.5 %all-gather.3 = f32[8,1,128]{2,1,0:T(1,128)S(1)} all-gather(f32[1,1,128]{2,1,0:T(1,128)S(1)} %bitcast.56), channel_id=3, replica_groups=mesh['gx'=2,'gy'=4,'gz'=4] {'gx','gz'}, dimensions={0}, use_global_device_ids=true | all-gather | bytes 4608 | tf_op jit(solution)/shard_map/all_gather | solution.py:11
  158.9 0.3 while.28
  159.2 0.7 copy.17
  (83 shorter events, 2.1 us)
Async XLA Ops:
  55.9 5.6 %copy-start = (s32[128]{0:T(128)S(1)}, s32[128]{0:T(128)}, u32[]{:S(2)}) copy-start(s32[128]{0:T(128)} %param.11) | copy-start | bytes 1540
  55.9 53.3 %all-to-all-start = ((f32[128,8,1,512]{0,1,2,3:T(8,128)}), f32[128,8,1,512]{0,1,2,3:T(8,128)S(1)}, u32[]{:S(2)}, u32[]{:S(2)}) async-start(f32[128,8,1,512]{0,1,2,3:T(8,128)} %copy.15), calls=%async_computation | async-start | bytes 4194304 | tf_op jit(solution)/shard_map/all_to_all | solution.py:67
